TPU v7x, 256 devices: a whole 4x4x8 slice. The times are simulated.
256 devices in a mesh: dp: 256 (over z, y, x, core).
Axes of the slice: x: 4, y: 4, z: 8, core: 2. Of those that a mesh axis runs over, the one named last changes fastest.
Arguments:
- grads: float32 [256, 1310720], P('dp'), may hold values from -24 to 24
- master: float32 [1310720], P('dp')
- moment1: float32 [1310720], P('dp'), may hold values from -4 to 4
- moment2: float32 [1310720], P('dp'), may hold values from 0.1 to 2
- tensor_rows: int32 [8], replicated, may hold values from 1 to 128, 256 in all
- step_count: int32 [1], replicated, may hold values from 1 to 19
Outputs:
- new_weights: bfloat16 [1310720], replicated
- new_master: float32 [1310720], P('dp')
- new_moment1: float32 [1310720], P('dp')
- new_moment2: float32 [1310720], P('dp')
All inputs are finite; a program needn't handle non-finite values.
Results may differ from a plain program's by a relative error of at most 0.001.
Values may be sent and summed in bfloat16 or wider, within the bound.
A program may use at most 64 MiB of HBM per device.

v0:
```python
import jax
import jax.numpy as jnp
from jax import lax
from jax.sharding import Mesh
from jax.sharding import PartitionSpec as P

D = 5120
DP = ("dp_0", "dp_1", "dp_2", "dp_3")


def in_blocks(value, dim, count):
    before, after = (value.shape[:dim], value.shape[dim + 1 :])
    return jnp.moveaxis(value.reshape(*before, count, -1, *after), dim, 0)


def summed_on_arrival(value, axis, dim):
    count = lax.axis_size(axis)
    tiles = lax.all_to_all(in_blocks(value, dim, count), axis, 0, 0, tiled=True)
    return jnp.sum(tiles.astype(jnp.float32), axis=0)


def sum_in_two_steps(value, axes, dim):
    far, near = axes
    own = summed_on_arrival(in_blocks(value, dim, lax.axis_size(far)), near, dim + 1)
    return jnp.sum(
        lax.all_to_all(own.astype(jnp.bfloat16), far, 0, 0, tiled=True).astype(jnp.float32), axis=0
    )


def from_everyone(value, axis):
    count = lax.axis_size(axis)
    return lax.all_to_all(
        jnp.broadcast_to(value[None], (count, *value.shape)), axis, 0, 0, tiled=True
    )


def taken_together(value, axis):
    everything = from_everyone(value, axis)
    return jnp.sum(everything, axis=0)


def by_axis(value, axes):
    far, near = axes
    return taken_together(taken_together(value, near), far)


def together(arrays, axis):
    ends = [0]
    for a in arrays:
        ends.append(ends[-1] + a.size)
    so_far = by_axis(jnp.concatenate([a.ravel() for a in arrays]), axis)
    return tuple((so_far[b:e].reshape(a.shape) for a, b, e in zip(arrays, ends, ends[1:])))


def joined_along(tiles, dim):
    tiles = jnp.moveaxis(tiles, 0, dim)
    dims = tiles.shape
    return tiles.reshape(*dims[:dim], dims[dim] * dims[dim + 1], *dims[dim + 2 :])


def gather_axes(value, axes, dim):
    far, near = axes
    initial = from_everyone(value, far)
    tiles = jnp.swapaxes(from_everyone(initial, near), 0, 1)
    return joined_along(tiles.reshape(-1, *value.shape), dim)


def tensor_sums(values, onehot, row_count, width):
    rows = values.reshape(row_count, width)
    row_sums = jnp.sum(rows * rows, axis=1)
    return jnp.sum(onehot * row_sums[:, None], axis=0)


def body(grads, master, moment1, moment2, tensor_rows, step_count):
    count = lax.axis_size(DP)
    me = lax.axis_index(DP)
    owned = master.shape[0]
    width = D
    row_count = owned // width
    ends = jnp.cumsum(tensor_rows)
    starts = ends - tensor_rows
    row_index = me * row_count + jnp.arange(row_count, dtype=jnp.int32)
    onehot = (
        (row_index[:, None] >= starts[None, :]) & (row_index[:, None] < ends[None, :])
    ).astype(jnp.float32)
    local_wsq = tensor_sums(master, onehot, row_count, width)
    flat = grads[0]
    summed = sum_in_two_steps(flat.astype(jnp.bfloat16), (("dp_0", "dp_1"), ("dp_2", "dp_3")), 0)
    grad = summed / jnp.float32(count)
    new_moment1 = 0.9 * moment1 + 0.1 * grad
    new_moment2 = 0.999 * moment2 + 0.001 * grad * grad
    steps = step_count[0].astype(jnp.float32)
    first = new_moment1 / (1.0 - jnp.power(jnp.float32(0.9), steps))
    second = new_moment2 / (1.0 - jnp.power(jnp.float32(0.999), steps))
    update = first / (jnp.sqrt(second) + 1e-06) + 0.1 * master
    local_usq = tensor_sums(update, onehot, row_count, width)
    wsq, usq = together((local_wsq, local_usq), (("dp_0", "dp_1"), ("dp_2", "dp_3")))
    ratio = jnp.sqrt(wsq / (usq + 1e-06))
    row_ratio = jnp.sum(onehot * ratio[None, :], axis=1)
    new_master = (
        master.reshape(row_count, width)
        - 0.2 * row_ratio[:, None] * update.reshape(row_count, width)
    ).reshape(owned)
    new_weights = gather_axes(
        new_master.astype(jnp.bfloat16), (("dp_0", "dp_1"), ("dp_2", "dp_3")), 0
    )
    return (new_weights, new_master, new_moment1, new_moment2)


def solution(mesh):
    torus = Mesh(mesh.devices.reshape(8, 4, 4, 2), ("dp_0", "dp_1", "dp_2", "dp_3"))
    placed = (P(DP, None), P(DP), P(DP), P(DP), P(), P())
    return jax.shard_map(
        body, mesh=torus, in_specs=placed, out_specs=(P(), P(DP), P(DP), P(DP)), check_vma=False
    )
```

profile of v0, /device:TPU:1, one launch (start us, length us, event | category | flops | bytes accessed | tf_op | source)
XLA Modules:
  0.0 214.0 jit_solution(16803403367068437620)
XLA Ops:
  0.6 56.9 %convert_reduce_fusion = bf16[1310720]{0:T(1024)(128)(2,1)} fusion(f32[1,1310720]{1,0:T(1,128)} %param.6), kind=kLoop, calls=%fused_computation | loop fusion | flops 1310720 | bytes 7864320 | tf_op jit(solution)/shard_map/convert_element_type | solution.py:88
  57.5 3.8 %convert_element_type.24 = bf16[32,8,5120]{2,1,0:T(8,128)(2,1)S(1)} reshape(bf16[1310720]{0:T(1024)(128)(2,1)} %convert_reduce_fusion) | data formatting | bytes 5242880 | tf_op jit(solution)/shard_map/convert_element_type | solution.py:88
  61.3 1.4 copy.17
  62.8 37.4 %all_to_all.37 = bf16[8,32,5120]{2,1,0:T(8,128)(2,1)S(1)} all-to-all(bf16[8,32,5120]{2,1,0:T(8,128)(2,1)S(1)} %copy.17), channel_id=1, replica_groups=mesh['dp_0'=8,'dp_1'=4,'dp_2'=4,'dp_3'=2] {'dp_2','dp_3'}, dimensions={0} | all-to-all | bytes 5242880 | tf_op jit(solution)/shard_map/all_to_all | solution.py:18
  100.2 0.5 reduce_sum.75
  100.7 0.6 broadcast.51
  101.3 0.9 reduce.12
  102.2 1.0 reshape.110
  103.1 11.1 %all-to-all-start.1 = ((bf16[32,2,2560]{2,1,0:T(2,128)(2,1)}), bf16[32,2,2560]{2,1,0:T(2,128)(2,1)S(1)}, u32[]{:S(2)}, u32[]{:S(2)}) async-start(bf16[32,2,2560]{2,1,0:T(2,128)(2,1)} %reshape.110), calls=%async_computation.1 | async-start | bytes 655360 | tf_op jit(solution)/shard_map/all_to_all | solution.py:26
  115.2 11.2 %all-to-all-done.1 = bf16[32,2,2560]{2,1,0:T(2,128)(2,1)S(1)} async-done(((bf16[32,2,2560]{2,1,0:T(2,128)(2,1)}), bf16[32,2,2560]{2,1,0:T(2,128)(2,1)S(1)}, u32[]{:S(2)}, u32[]{:S(2)}) %all-to-all-start.1) | async-done | bytes 327712 | tf_op jit(solution)/shard_map/all_to_all | solution.py:26
  126.7 0.6 convert_reduce_fusion.1
  127.3 1.3 multiply_reduce_fusion
  128.6 0.6 broadcast_select_fusion.1
  129.2 0.7 broadcast_select_fusion
  129.9 9.8 %all_to_all.38 = f32[8,1,16]{2,1,0:T(1,128)S(1)} all-to-all(f32[8,1,16]{2,1,0:T(1,128)S(1)} %broadcast_in_dim.10), channel_id=1, replica_groups=mesh['dp_0'=8,'dp_1'=4,'dp_2'=4,'dp_3'=2] {'dp_2','dp_3'}, dimensions={0} | all-to-all | bytes 1024 | tf_op jit(solution)/shard_map/all_to_all | solution.py:32
  139.7 12.3 %all_to_all.39 = f32[32,1,16]{2,1,0:T(1,128)S(1)} all-to-all(f32[32,1,16]{2,1,0:T(1,128)S(1)} %broadcast_in_dim.11), channel_id=1, replica_groups=mesh['dp_0'=8,'dp_1'=4,'dp_2'=4,'dp_3'=2] {'dp_0','dp_1'}, dimensions={0} | all-to-all | bytes 4096 | tf_op jit(solution)/shard_map/all_to_all | solution.py:32
  152.1 0.7 select_reduce_fusion
  153.5 0.6 fusion
  154.1 0.3 broadcast_in_dim.12
  154.4 2.6 %reduce.13 = bf16[32,5120]{1,0:T(8,128)(2,1)S(1)} reduce(bf16[32,1,5120]{2,1,0:T(2,128)(2,1)S(1)} %broadcast_in_dim.12, bf16[]{:T(256)} %broadcast.51), dimensions={1}, to_apply=%broadcast_in_dim.12.reduce_sub_computation | reduce | bytes 655362 | tf_op jit(solution)/shard_map/broadcast_in_dim | solution.py:33
  157.3 14.1 %all_to_all.40 = bf16[32,2,2560]{2,1,0:T(2,128)(2,1)S(1)} all-to-all(bf16[32,2,2560]{2,1,0:T(2,128)(2,1)S(1)} %reshape.112), channel_id=1, replica_groups=mesh['dp_0'=8,'dp_1'=4,'dp_2'=4,'dp_3'=2] {'dp_0','dp_1'}, dimensions={0} | all-to-all | bytes 655360 | tf_op jit(solution)/shard_map/all_to_all | solution.py:32
  172.1 38.5 %all_to_all.41 = bf16[8,32,5120]{2,1,0:T(8,128)(2,1)S(1)} all-to-all(bf16[8,32,5120]{2,1,0:T(8,128)(2,1)S(1)} %broadcast_in_dim.14), channel_id=1, replica_groups=mesh['dp_0'=8,'dp_1'=4,'dp_2'=4,'dp_3'=2] {'dp_2','dp_3'}, dimensions={0} | all-to-all | bytes 5242880 | tf_op jit(solution)/shard_map/all_to_all | solution.py:32
  210.6 1.4 copy.29
  212.0 2.0 copy.26
  (19 shorter events, 1.5 us)
Async XLA Ops:
  100.2 14.8 %copy-start.3 = (s32[8]{0:T(128)S(1)}, s32[8]{0:T(128)}, u32[]{:S(2)}) copy-start(s32[8]{0:T(128)} %param.10) | copy-start | bytes 100
  100.2 27.1 %copy-start = (f32[5120]{0:T(1024)S(1)}, f32[5120]{0:T(1024)}, u32[]{:S(2)}) copy-start(f32[5120]{0:T(1024)} %param.7) | copy-start | bytes 61444
  100.2 27.1 %copy-start.1 = (f32[5120]{0:T(1024)S(1)}, f32[5120]{0:T(1024)}, u32[]{:S(2)}) copy-start(f32[5120]{0:T(1024)} %param.9) | copy-start | bytes 61444
  100.2 27.1 %copy-start.2 = (f32[5120]{0:T(1024)S(1)}, f32[5120]{0:T(1024)}, u32[]{:S(2)}) copy-start(f32[5120]{0:T(1024)} %param.8) | copy-start | bytes 61444
  103.1 23.3 %all-to-all-start.1 = ((bf16[32,2,2560]{2,1,0:T(2,128)(2,1)}), bf16[32,2,2560]{2,1,0:T(2,128)(2,1)S(1)}, u32[]{:S(2)}, u32[]{:S(2)}) async-start(bf16[32,2,2560]{2,1,0:T(2,128)(2,1)} %reshape.110), calls=%async_computation.1 | async-start | bytes 655360 | tf_op jit(solution)/shard_map/all_to_all | solution.py:26
where the time goes:
time: 215 us; the launch traced here: 214 us
  blocking collectives  112 us (52%)
  other arithmetic  65.6 us (31%)
  local copies, waits for them, and re-layouts  11.8 us (5%)
  waiting for transfers between devices  11.2 us (5%)
  starting transfers between devices  11.1 us (5%)
  between operations  2.17 us (1%)
    all_to_all x4, blocking collectives, from_everyone(): lax.all_to_all(jnp.broadcast_to(value[None], (count, *value.shape)), axis...  74.7 us
    convert_element_type x1, other arithmetic, body(): flat.astype(jnp.bfloat16)  56.9 us
    all_to_all x1, blocking collectives, summed_on_arrival(): tiles = lax.all_to_all(in_blocks(value, dim, count), axis, 0, 0, tiled=True)  37.4 us
    all_to_all x1, waiting for transfers between devices, sum_in_two_steps(): lax.all_to_all(own.astype(jnp.bfloat16), far, 0, 0, tiled=True)  11.2 us
    all_to_all x1, starting transfers between devices, sum_in_two_steps(): lax.all_to_all(own.astype(jnp.bfloat16), far, 0, 0, tiled=True)  11.1 us
  transfers between devices with their start and end apart: 1, of which 1 were waited for; matrix products, arithmetic and copies ran while one was open for 0% of the time, Pallas kernels for 0%

commit v1 on v0

v1 whole, which is shorter than its diff:
```python
import jax
import jax.numpy as jnp
from jax import lax
from jax.experimental import pallas as pl
from jax.experimental.pallas import tpu as pltpu
from jax.sharding import Mesh
from jax.sharding import PartitionSpec as P

AXES = ("z", "y", "x", "c")
NZ, NY, NX, NC = 8, 4, 4, 2
NSEG = 8
TILE = (5, 8, 128)
MESH_ID = pl.DeviceIdType.MESH
F32 = jnp.float32
BF16 = jnp.bfloat16


def power(base, t):
    out = jnp.float32(1.0)
    square = jnp.float32(base)
    for bit in range(5):
        out = jnp.where((t >> bit) & 1 == 1, out * square, out)
        square = square * square
    return out


def kernel(
    grads, master, moment1, moment2, rows_ref, step_ref,
    weights, out_master, out_m1, out_m2,
    gbuf, psnd, prcv, own0, own, fwd, fin, snd2, p2snd, p2rcv, col, zsnd, zrcv,
    m1v, m2v, mz, uz, ar_a, ar_b, nmv, gat,
    ld_sem, ps_sem, pr_sem, p1s_sem, p1r_sem, p2s_sem, p2r_sem,
    zs_sem, zr_sem, ms_sem, mr_sem, us_sem, ur_sem, as_sem, ar_sem, bs_sem, br_sem,
    g2s_sem, g2r_sem, g1s_sem, g1r_sem, in_sem, o_sem, ds_sem, dr_sem, ow_sem,
):
    z, y, x, c = (lax.axis_index(a) for a in AXES)
    zc = z * NC + c
    yx = y * NX + x
    other = 1 - c

    def zc_peer(i):
        t = lax.rem(zc + i, NZ * NC)
        return {"z": t // NC, "c": lax.rem(t, NC)}

    def yx_peer(i):
        t = lax.rem(yx + i, NY * NX)
        return {"y": t // NX, "x": lax.rem(t, NX)}

    barrier = pltpu.get_barrier_semaphore()

    def greet(i, carry):
        pl.semaphore_signal(barrier, inc=1, device_id=zc_peer(i), device_id_type=MESH_ID)
        pl.semaphore_signal(barrier, inc=1, device_id=yx_peer(i), device_id_type=MESH_ID)
        return carry

    lax.fori_loop(1, 16, greet, 0)

    firsts, seconds = (x, y), (y, x)
    first_axis, second_axis = ("x", "y"), ("y", "x")

    def place(p, k, j):
        t1, t2 = lax.rem(firsts[p] + k, 4), lax.rem(seconds[p] + j, 4)
        return (pl.ds(4 * p, 4), t2, t1) if p == 0 else (pl.ds(4 * p, 4), t1, t2)

    def remote(src, dst, ssem, rsem, dev):
        return pltpu.make_async_remote_copy(
            src_ref=src, dst_ref=dst, send_sem=ssem, recv_sem=rsem,
            device_id=dev, device_id_type=MESH_ID,
        )

    order = [(p, d) for d in (2, 1, 3, 0) for p in (0, 1)]
    for n, (p, d) in enumerate(order):
        for j in range(4):
            pltpu.make_async_copy(grads.at[place(p, d, j)], gbuf.at[p, d, j], ld_sem.at[p, d]).start()
        if n == 1:
            pltpu.make_async_copy(master, mz.at[z], in_sem.at[0]).start()
    pltpu.make_async_copy(moment1, m1v, in_sem.at[1]).start()
    pltpu.make_async_copy(moment2, m2v, in_sem.at[2]).start()

    pair = {
        (p, d): remote(psnd.at[p, d], prcv.at[p, d], ps_sem.at[p, d], pr_sem.at[p, d], {"c": other})
        for p, d in order
    }
    for n, (p, d) in enumerate(order):
        pltpu.make_async_copy(gbuf.at[p, d], gbuf.at[p, d], ld_sem.at[p, d]).wait()

        def cast(j, carry, p=p, d=d):
            psnd[p, d, j] = gbuf[p, d, j, :, other].astype(BF16)
            return carry

        lax.fori_loop(0, 4, cast, 0)
        if n == 0:
            pl.semaphore_wait(barrier, 30)
        pair[p, d].start()

    pltpu.make_async_copy(master, mz.at[z], in_sem.at[0]).wait()
    far_first = (4, 3, 5, 2, 6, 1, 7)

    def z_sends(src_of, dst, ssem, rsem):
        for d in far_first:
            t = lax.rem(z + d, NZ)
            remote(src_of(t), dst, ssem, rsem, {"z": t}).start()

    z_sends(lambda t: mz.at[z], mz.at[z], ms_sem, mr_sem)

    ring = {}
    for p in (0, 1):
        a, i1 = first_axis[p], firsts[p]
        right, left = {a: lax.rem(i1 + 1, 4)}, {a: lax.rem(i1 + 3, 4)}
        lo, hi = pl.ds(0, 2), pl.ds(2, 2)
        ring[p] = [
            remote(own.at[p, 1, lo], fwd.at[p, 0], p1s_sem.at[p, 0], p1r_sem.at[p, 0], right),
            remote(own.at[p, 1, hi], fwd.at[p, 1], p1s_sem.at[p, 1], p1r_sem.at[p, 1], left),
            remote(own.at[p, 0, hi], fin.at[p, 0, hi], p1s_sem.at[p, 2], p1r_sem.at[p, 2], right),
            remote(own.at[p, 2, lo], fin.at[p, 1, lo], p1s_sem.at[p, 3], p1r_sem.at[p, 3], left),
            remote(snd2.at[p, 0], fin.at[p, 0, lo], p1s_sem.at[p, 4], p1r_sem.at[p, 4], right),
            remote(snd2.at[p, 1], fin.at[p, 1, hi], p1s_sem.at[p, 5], p1r_sem.at[p, 5], left),
        ]
    for p, d in order:
        pair[p, d].wait_recv()

        def add(j, carry, p=p, d=d):
            total = gbuf[p, d, j, :, c] + prcv[p, d, j].astype(F32)
            if d == 0:
                own0[p, j] = total
            else:
                own[p, d - 1, j] = total.astype(BF16)
            return carry

        lax.fori_loop(0, 4, add, 0)
        if d == 2:
            ring[p][0].start()
            ring[p][1].start()
        elif d == 1:
            ring[p][2].start()
        elif d == 3:
            ring[p][3].start()
    for p in (0, 1):
        for way, (slot, base) in enumerate(((0, 0), (2, 2))):
            ring[p][way].wait_recv()

            def onward(j, carry, p=p, way=way, slot=slot, base=base):
                total = own[p, slot, base + j].astype(F32) + fwd[p, way, j].astype(F32)
                snd2[p, way, j] = total.astype(BF16)
                return carry

            lax.fori_loop(0, 2, onward, 0)
            ring[p][4 + way].start()

    across = {
        (p, j): remote(
            p2snd.at[p, j - 1], p2rcv.at[p, j - 1], p2s_sem.at[p, j - 1], p2r_sem.at[p, j - 1],
            {second_axis[p]: lax.rem(seconds[p] + j, 4)},
        )
        for p in (0, 1) for j in (1, 2, 3)
    }
    for p in (0, 1):
        for n in (2, 3, 4, 5):
            ring[p][n].wait_recv()
        for j in (2, 1, 3, 0):
            total = own0[p, j] + fin[p, 0, j].astype(F32) + fin[p, 1, j].astype(F32)
            if j:
                p2snd[p, j - 1] = total.astype(BF16)
                across[p, j].start()
            else:
                col[p] = total
    for p in (0, 1):
        for j in (1, 3, 2):
            across[p, j].wait_recv()
        total = col[p]
        for j in (1, 2, 3):
            total = total + p2rcv[p, j - 1].astype(F32)
        col[p] = total
        zsnd[pl.ds(4 * p, 4)] = total.astype(BF16)

    z_sends(lambda t: zsnd.at[t], zrcv.at[z], zs_sem, zr_sem)

    lane = lax.broadcasted_iota(jnp.int32, (1, 128), 1)
    starts = jnp.zeros((1, 128), jnp.int32)
    ends = jnp.zeros((1, 128), jnp.int32)
    edge = jnp.int32(0)
    for k in range(NSEG):
        starts = jnp.where(lane == k, edge, starts)
        edge = edge + rows_ref[k]
        ends = jnp.where(lane == k, edge, ends)
    my_row = (z * NY * NX + yx) * NC + c
    my_hot = jnp.where((my_row >= starts) & (my_row < ends), 1.0, 0.0).astype(F32)
    col_row = (lax.broadcasted_iota(jnp.int32, (NZ, 128), 0) * (NY * NX) + yx) * NC + c
    col_hot = jnp.where((col_row >= starts) & (col_row < ends), 1.0, 0.0).astype(F32)
    t = step_ref[0]
    scale1 = 1.0 - power(0.9, t)
    scale2 = 1.0 - power(0.999, t)
    mine = mz[z]
    my_wsq = jnp.sum(jnp.sum(jnp.sum(mine * mine, axis=0), axis=0, keepdims=True), axis=1, keepdims=True)
    pltpu.make_async_copy(moment1, m1v, in_sem.at[1]).wait()
    pltpu.make_async_copy(moment2, m2v, in_sem.at[2]).wait()

    def z_all(ref, ssem, rsem):
        return remote(ref.at[pl.ds(0, 7)], ref.at[pl.ds(0, 7)], ssem, rsem, {"z": lax.rem(z + 1, NZ)})

    z_all(zrcv, zs_sem, zr_sem).wait_recv()
    total = col[z // 4, lax.rem(z, 4)]
    for i in range(1, NZ):
        total = total + zrcv[lax.rem(z + i, NZ)].astype(F32)
    grad = total / jnp.float32(256)
    m1 = 0.9 * m1v[...] + 0.1 * grad
    m2 = 0.999 * m2v[...] + 0.001 * grad * grad
    update = (m1 / scale1) / (jnp.sqrt(m2 / scale2) + 1e-6) + 0.1 * mine
    my_usq = jnp.sum(jnp.sum(jnp.sum(update * update, axis=0), axis=0, keepdims=True), axis=1, keepdims=True)
    ar_a[zc, 0:1] = my_hot * my_usq
    ar_a[zc, 1:2] = my_hot * my_wsq
    for i in range(1, 16):
        remote(ar_a.at[zc], ar_a.at[zc], as_sem, ar_sem, zc_peer(i)).start()
    uz[z] = update
    z_sends(lambda t: uz.at[z], uz.at[z], us_sem, ur_sem)
    m1v[...] = m1
    m2v[...] = m2
    pltpu.make_async_copy(m1v, out_m1, ow_sem.at[0]).start()
    pltpu.make_async_copy(m2v, out_m2, ow_sem.at[1]).start()

    def few(ref, ssem, rsem, dev):
        return remote(ref.at[pl.ds(0, 15)], ref.at[pl.ds(0, 15)], ssem, rsem, dev)

    few(ar_a, as_sem, ar_sem, zc_peer(1)).wait_recv()
    ar_b[yx] = jnp.sum(ar_a[...], axis=0)
    for i in range(1, 16):
        remote(ar_b.at[yx], ar_b.at[yx], bs_sem, br_sem, yx_peer(i)).start()
    z_all(mz, ms_sem, mr_sem).wait_recv()
    z_all(uz, us_sem, ur_sem).wait_recv()
    few(ar_b, bs_sem, br_sem, yx_peer(1)).wait_recv()
    sums = jnp.sum(ar_b[...], axis=0)
    ratio = jnp.sqrt(sums[1:2] / (sums[0:1] + 1e-6))
    col_ratio = 0.2 * jnp.sum(col_hot * ratio, axis=1, keepdims=True)
    my_ratio = 0.2 * jnp.sum(my_hot * ratio, axis=1, keepdims=True)
    for i in range(NZ):
        factor = jnp.broadcast_to(col_ratio[i : i + 1], (8, 128))
        gat[i // 4, 0, 0, i % 4] = (mz[i] - factor * uz[i]).astype(BF16)

    def store(p, k, j):
        spot = place(p, k, j)
        pltpu.make_async_copy(gat.at[p, k, j], weights.at[(*spot, c)], o_sem).start()
        remote(gat.at[p, k, j], weights.at[(*spot, c)], ds_sem, dr_sem, {"c": other}).start()

    spread = {
        (p, d): remote(
            gat.at[p, 0, 0], gat.at[p, 0, 4 - d], g2s_sem.at[p, d - 1], g2r_sem.at[p, d - 1],
            {second_axis[p]: lax.rem(seconds[p] + d, 4)},
        )
        for p in (0, 1) for d in (1, 2, 3)
    }

    def hop(p, way, src_k, dst_k, j, n):
        a, i1 = first_axis[p], firsts[p]
        dev = {a: lax.rem(i1 + (1 if way == 0 else 3), 4)}
        return remote(
            gat.at[p, src_k, j], gat.at[p, dst_k, j], g1s_sem.at[p, way, n], g1r_sem.at[p, way, n], dev
        )

    near = {(p, w, j): hop(p, w, 0, (3, 1)[w], j, j) for p in (0, 1) for w in (0, 1) for j in range(4)}
    passed = ((0, 1), (3, 2))
    second = {
        (p, w, j): hop(p, w, (3, 1)[w], 2, j, 4 + n)
        for p in (0, 1) for w in (0, 1) for n, j in enumerate(passed[w])
    }
    for p in (0, 1):
        for d in (1, 3, 2):
            spread[p, d].start()
        for w in (0, 1):
            near[p, w, 0].start()
    nmv[...] = mine - jnp.broadcast_to(my_ratio, (8, 128)) * update
    pltpu.make_async_copy(nmv, out_master, ow_sem.at[2]).start()
    for p in (0, 1):
        store(p, 0, 0)
    for j in (1, 3, 2):
        for p in (0, 1):
            spread[p, 4 - j].wait_recv()
            for w in (0, 1):
                near[p, w, j].start()
            store(p, 0, j)
        if j == 1:
            for p in (0, 1):
                for w in (0, 1):
                    near[p, w, 0].wait_recv()
                    if 0 in passed[w]:
                        second[p, w, 0].start()
                    store(p, (3, 1)[w], 0)
    for j in (1, 3, 2):
        for p in (0, 1):
            for w in (0, 1):
                near[p, w, j].wait_recv()
                if j in passed[w]:
                    second[p, w, j].start()
                store(p, (3, 1)[w], j)
    for n in (0, 1):
        for p in (0, 1):
            for w in (0, 1):
                j = passed[w][n]
                second[p, w, j].wait_recv()
                store(p, 2, j)

    for p, d in order:
        pair[p, d].wait_send()
    for p in (0, 1):
        for copy in ring[p]:
            copy.wait_send()
    for group in (across, spread, near, second):
        for copy in group.values():
            copy.wait_send()
    z_all(mz, ms_sem, mr_sem).wait_send()
    z_all(zrcv, zs_sem, zr_sem).wait_send()
    z_all(uz, us_sem, ur_sem).wait_send()
    few(ar_a, as_sem, ar_sem, zc_peer(1)).wait_send()
    few(ar_b, bs_sem, br_sem, yx_peer(1)).wait_send()
    pltpu.make_async_copy(m1v, out_m1, ow_sem.at[0]).wait()
    pltpu.make_async_copy(m2v, out_m2, ow_sem.at[1]).wait()
    pltpu.make_async_copy(nmv, out_master, ow_sem.at[2]).wait()
    half = weights.at[:, :, :, c]
    pltpu.make_async_copy(half, half, o_sem).wait()
    both = remote(half, half, ds_sem, dr_sem, {"c": other})
    both.wait_send()
    both.wait_recv()


def body(grads, master, moment1, moment2, tensor_rows, step_count):
    any_space = pl.BlockSpec(memory_space=pl.ANY)
    smem = pl.BlockSpec(memory_space=pltpu.SMEM)
    full = (NZ, NY, NX, NC, *TILE)
    block = jax.ShapeDtypeStruct(TILE, F32)
    dma = pltpu.SemaphoreType.DMA
    vm = pltpu.VMEM
    scratch = [
        vm((2, 4, 4, 4, 2, *TILE), F32),
        vm((2, 4, 4, 4, *TILE), BF16),
        vm((2, 4, 4, 4, *TILE), BF16),
        vm((2, 4, 4, *TILE), F32),
        vm((2, 3, 4, 4, *TILE), BF16),
        vm((2, 2, 2, 4, *TILE), BF16),
        vm((2, 2, 4, 4, *TILE), BF16),
        vm((2, 2, 2, 4, *TILE), BF16),
        vm((2, 3, 4, *TILE), BF16),
        vm((2, 3, 4, *TILE), BF16),
        vm((2, 4, *TILE), F32),
        vm((NZ, *TILE), BF16),
        vm((NZ, *TILE), BF16),
        vm(TILE, F32),
        vm(TILE, F32),
        vm((NZ, *TILE), F32),
        vm((NZ, *TILE), F32),
        vm((16, 2, 128), F32),
        vm((16, 2, 128), F32),
        vm(TILE, F32),
        vm((2, 4, 4, 4, *TILE), BF16),
        dma((2, 4)), dma((2, 4)), dma((2, 4)), dma((2, 6)), dma((2, 6)), dma((2, 3)), dma((2, 3)),
        dma, dma, dma, dma, dma, dma, dma, dma, dma, dma,
        dma((2, 3)), dma((2, 3)), dma((2, 2, 6)), dma((2, 2, 6)), dma((3,)), dma, dma, dma, dma((3,)),
    ]
    weights, new_master, new_m1, new_m2 = pl.pallas_call(
        kernel,
        out_shape=(jax.ShapeDtypeStruct(full, BF16), block, block, block),
        in_specs=[any_space] * 4 + [smem] * 2,
        out_specs=(any_space,) * 4,
        scratch_shapes=scratch,
        compiler_params=pltpu.CompilerParams(
            collective_id=0, has_side_effects=True, vmem_limit_bytes=40 * 1024 * 1024
        ),
    )(
        grads.reshape(full), master.reshape(TILE), moment1.reshape(TILE), moment2.reshape(TILE),
        tensor_rows, step_count,
    )
    return (weights.reshape(-1), new_master.reshape(-1), new_m1.reshape(-1), new_m2.reshape(-1))


def solution(mesh):
    torus = Mesh(mesh.devices.reshape(NZ, NY, NX, NC), AXES)
    placed = (P(AXES, None), P(AXES), P(AXES), P(AXES), P(), P())
    return jax.shard_map(
        body, mesh=torus, in_specs=placed, out_specs=(P(), P(AXES), P(AXES), P(AXES)), check_vma=False
    )
```

time: 215 us -> 64.9 us (0.30)
  blocking collectives: 112 us -> 0 us
  other arithmetic: 65.6 us -> 0 us
  Pallas kernels: 0 us -> 54.6 us
  waiting for transfers between devices: 11.2 us -> 0 us
  starting transfers between devices: 11.1 us -> 0 us
  local copies, waits for them, and re-layouts: 11.8 us -> 8.73 us
    all_to_all x5 -> x0, blocking collectives: 112 us -> none  [the longest x4 74.7 us: from_everyone(): lax.all_to_all(jnp.broadcast_to(value[None], (count, *value.shape)), axis...]
    convert_element_type x2 -> x0, other arithmetic: 57.5 us -> none  [the longest x1 56.9 us: body(): flat.astype(jnp.bfloat16)]
    pallas_call x0 -> x1, Pallas kernels: none -> 54.6 us  [body(): pl.pallas_call(kernel, out_shape=(jax.ShapeDtypeStruct(full, BF16), block...]
    all_to_all x1 -> x0, waiting for transfers between devices: 11.2 us -> none  [sum_in_two_steps(): lax.all_to_all(own.astype(jnp.bfloat16), far, 0, 0, tiled=True)]
    all_to_all x1 -> x0, starting transfers between devices: 11.1 us -> none  [sum_in_two_steps(): lax.all_to_all(own.astype(jnp.bfloat16), far, 0, 0, tiled=True)]
    unnamed x14, local copies, waits for them, and re-layouts: 3.87 us -> 8.73 us
    convert_element_type x1 -> x0, local copies, waits for them, and re-layouts: 3.77 us -> none  [body(): flat.astype(jnp.bfloat16)]
    reduce_sum x6 -> x0, other arithmetic: 3.09 us -> none  [the longest x1 1.26 us: tensor_sums(): row_sums = jnp.sum(rows * rows, axis=1)]
  transfers between devices with their start and end apart: 1 -> 0, of which waited for: 1 -> 0; matrix products, arithmetic and copies ran while one was open for 0% -> 0% of each run, Pallas kernels for 0% -> 0%
where the time goes in v1:
time: 64.9 us; the launch traced here: 64.6 us
  Pallas kernels  54.6 us (84%)
  local copies, waits for them, and re-layouts  8.73 us (13%)
  between operations  1.3 us (2%)
    pallas_call x1, Pallas kernels, body(): pl.pallas_call(kernel, out_shape=(jax.ShapeDtypeStruct(full, BF16), block...  54.6 us
    unnamed x14, local copies, waits for them, and re-layouts  8.73 us

profile of v1, /device:TPU:1, one launch (start us, length us, event | category | flops | bytes accessed | tf_op | source)
XLA Modules:
  0.0 64.6 jit_solution(10999465486899254508)
XLA Ops:
  1.3 0.0 copy-start
  1.3 2.5 %copy-done = f32[1,1310720]{1,0:T(1,128)S(1)} copy-done((f32[1,1310720]{1,0:T(1,128)S(1)}, f32[1,1310720]{1,0:T(1,128)}, u32[]{:S(2)}) %copy-start) | copy-done | bytes 5242904
  3.8 0.0 copy-start.1
  3.8 0.7 %copy-done.1 = f32[5120]{0:T(1024)S(1)} copy-done((f32[5120]{0:T(1024)S(1)}, f32[5120]{0:T(1024)}, u32[]{:S(2)}) %copy-start.1) | copy-done | bytes 20504
  4.5 0.0 copy-start.2
  4.5 0.7 %copy-done.2 = f32[5120]{0:T(1024)S(1)} copy-done((f32[5120]{0:T(1024)S(1)}, f32[5120]{0:T(1024)}, u32[]{:S(2)}) %copy-start.2) | copy-done | bytes 20504
  5.2 0.0 copy-start.3
  5.2 0.7 %copy-done.3 = f32[5120]{0:T(1024)S(1)} copy-done((f32[5120]{0:T(1024)S(1)}, f32[5120]{0:T(1024)}, u32[]{:S(2)}) %copy-start.3) | copy-done | bytes 20504
  6.0 0.0 copy-start.4
  6.0 0.7 %copy-done.4 = s32[8]{0:T(128)S(1)} copy-done((s32[8]{0:T(128)S(1)}, s32[8]{0:T(128)}, u32[]{:S(2)}) %copy-start.4) | copy-done | bytes 56
  6.6 54.6 %shard_map.93 = (bf16[8,4,4,2,5,8,128]{6,5,4,3,2,1,0:T(8,128)(2,1)S(1)}, f32[5,8,128]{2,1,0:T(8,128)S(1)}, f32[5,8,128]{2,1,0:T(8,128)S(1)}, f32[5,8,128]{2,1,0:T(8,128)S(1)}) custom-call(f32[8,4,4,2,5,8,128]{6,5,4,3,2,1,0:T(8,128)S(1)} %bitcast.8, f32[5,8,128]{2,1,0:T(8,128)S(1)} %bitcast.10, f32[5,8,128]{2,1,0:T(8,128)S(1)} %bitcast.11, ...), custom_call_target="tpu_custom_call" | custom-call | tf_op jit(solution)/shard_map/pallas_call | solution.py:357
  61.2 1.6 %copy.15 = bf16[1310720]{0:T(1024)(128)(2,1)} copy(bf16[1310720]{0:T(1024)(128)(2,1)S(1)} %bitcast.9) | data formatting | bytes 5242880
  62.8 0.6 copy.16
  63.4 0.6 copy.17
  64.0 0.6 copy.18
Async XLA Ops:
  1.3 2.5 %copy-start = (f32[1,1310720]{1,0:T(1,128)S(1)}, f32[1,1310720]{1,0:T(1,128)}, u32[]{:S(2)}) copy-start(f32[1,1310720]{1,0:T(1,128)} %param.6) | copy-start | bytes 15728644
  3.8 0.7 %copy-start.1 = (f32[5120]{0:T(1024)S(1)}, f32[5120]{0:T(1024)}, u32[]{:S(2)}) copy-start(f32[5120]{0:T(1024)} %param.7) | copy-start | bytes 61444
  4.5 0.7 %copy-start.2 = (f32[5120]{0:T(1024)S(1)}, f32[5120]{0:T(1024)}, u32[]{:S(2)}) copy-start(f32[5120]{0:T(1024)} %param.8) | copy-start | bytes 61444
  5.2 0.7 %copy-start.3 = (f32[5120]{0:T(1024)S(1)}, f32[5120]{0:T(1024)}, u32[]{:S(2)}) copy-start(f32[5120]{0:T(1024)} %param.9) | copy-start | bytes 61444
  6.0 0.7 %copy-start.4 = (s32[8]{0:T(128)S(1)}, s32[8]{0:T(128)}, u32[]{:S(2)}) copy-start(s32[8]{0:T(128)} %rows_ref.1) | copy-start | bytes 100

commit v2 on v1

--- a/solution.py
+++ b/solution.py
@@ -25,13 +25,13 @@
 
 
 def kernel(
-    grads, master, moment1, moment2, rows_ref, step_ref,
+    grads, master, moment1, moment2, rows_hbm, step_ref,
     weights, out_master, out_m1, out_m2,
     gbuf, psnd, prcv, own0, own, fwd, fin, snd2, p2snd, p2rcv, col, zsnd, zrcv,
-    m1v, m2v, mz, uz, ar_a, ar_b, nmv, gat,
+    rows_ref, m1v, m2v, mz, uz, ar_a, ar_b,
     ld_sem, ps_sem, pr_sem, p1s_sem, p1r_sem, p2s_sem, p2r_sem,
     zs_sem, zr_sem, ms_sem, mr_sem, us_sem, ur_sem, as_sem, ar_sem, bs_sem, br_sem,
-    g2s_sem, g2r_sem, g1s_sem, g1r_sem, in_sem, o_sem, ds_sem, dr_sem, ow_sem,
+    g2s_sem, g2r_sem, g1s_sem, g1r_sem, in_sem, ds_sem, dr_sem,
 ):
     z, y, x, c = (lax.axis_index(a) for a in AXES)
     zc = z * NC + c
@@ -76,6 +76,7 @@
             pltpu.make_async_copy(master, mz.at[z], in_sem.at[0]).start()
     pltpu.make_async_copy(moment1, m1v, in_sem.at[1]).start()
     pltpu.make_async_copy(moment2, m2v, in_sem.at[2]).start()
+    pltpu.make_async_copy(rows_hbm, rows_ref, in_sem.at[3]).start()
 
     pair = {
         (p, d): remote(psnd.at[p, d], prcv.at[p, d], ps_sem.at[p, d], pr_sem.at[p, d], {"c": other})
@@ -175,6 +176,7 @@
 
     z_sends(lambda t: zsnd.at[t], zrcv.at[z], zs_sem, zr_sem)
 
+    pltpu.make_async_copy(rows_hbm, rows_ref, in_sem.at[3]).wait()
     lane = lax.broadcasted_iota(jnp.int32, (1, 128), 1)
     starts = jnp.zeros((1, 128), jnp.int32)
     ends = jnp.zeros((1, 128), jnp.int32)
@@ -213,10 +215,8 @@
         remote(ar_a.at[zc], ar_a.at[zc], as_sem, ar_sem, zc_peer(i)).start()
     uz[z] = update
     z_sends(lambda t: uz.at[z], uz.at[z], us_sem, ur_sem)
-    m1v[...] = m1
-    m2v[...] = m2
-    pltpu.make_async_copy(m1v, out_m1, ow_sem.at[0]).start()
-    pltpu.make_async_copy(m2v, out_m2, ow_sem.at[1]).start()
+    out_m1[...] = m1
+    out_m2[...] = m2
 
     def few(ref, ssem, rsem, dev):
         return remote(ref.at[pl.ds(0, 15)], ref.at[pl.ds(0, 15)], ssem, rsem, dev)
@@ -234,68 +234,67 @@
     my_ratio = 0.2 * jnp.sum(my_hot * ratio, axis=1, keepdims=True)
     for i in range(NZ):
         factor = jnp.broadcast_to(col_ratio[i : i + 1], (8, 128))
-        gat[i // 4, 0, 0, i % 4] = (mz[i] - factor * uz[i]).astype(BF16)
+        weights[i, y, x, c] = (mz[i] - factor * uz[i]).astype(BF16)
+
+    def spot(p, k, j):
+        return weights.at[(*place(p, k, j), c)]
 
     def store(p, k, j):
-        spot = place(p, k, j)
-        pltpu.make_async_copy(gat.at[p, k, j], weights.at[(*spot, c)], o_sem).start()
-        remote(gat.at[p, k, j], weights.at[(*spot, c)], ds_sem, dr_sem, {"c": other}).start()
-
-    spread = {
-        (p, d): remote(
-            gat.at[p, 0, 0], gat.at[p, 0, 4 - d], g2s_sem.at[p, d - 1], g2r_sem.at[p, d - 1],
+        remote(spot(p, k, j), spot(p, k, j), ds_sem, dr_sem, {"c": other}).start()
+
+    def spread_copy(p, j, d):
+        return remote(
+            spot(p, 0, j), spot(p, 0, j), g2s_sem.at[p, d - 1], g2r_sem.at[p, d - 1],
             {second_axis[p]: lax.rem(seconds[p] + d, 4)},
         )
-        for p in (0, 1) for d in (1, 2, 3)
-    }
-
-    def hop(p, way, src_k, dst_k, j, n):
-        a, i1 = first_axis[p], firsts[p]
-        dev = {a: lax.rem(i1 + (1 if way == 0 else 3), 4)}
-        return remote(
-            gat.at[p, src_k, j], gat.at[p, dst_k, j], g1s_sem.at[p, way, n], g1r_sem.at[p, way, n], dev
-        )
-
-    near = {(p, w, j): hop(p, w, 0, (3, 1)[w], j, j) for p in (0, 1) for w in (0, 1) for j in range(4)}
+
+    def hop(p, way, k, j, n):
+        dev = {first_axis[p]: lax.rem(firsts[p] + (1 if way == 0 else 3), 4)}
+        return remote(spot(p, k, j), spot(p, k, j), g1s_sem.at[p, way, n], g1r_sem.at[p, way, n], dev)
+
     passed = ((0, 1), (3, 2))
-    second = {
-        (p, w, j): hop(p, w, (3, 1)[w], 2, j, 4 + n)
-        for p in (0, 1) for w in (0, 1) for n, j in enumerate(passed[w])
-    }
+    pd = [(p, d) for p in (0, 1) for d in (1, 2, 3)]
+    pwj = [(p, w, j) for p in (0, 1) for w in (0, 1) for j in range(4)]
+    pwn = [(p, w, n) for p in (0, 1) for w in (0, 1) for n in (0, 1)]
+    spread_sent = {(p, d): spread_copy(p, 0, d) for p, d in pd}
+    spread_here = {(p, 4 - d): spread_copy(p, 4 - d, d) for p, d in pd}
+    near_sent = {(p, w, j): hop(p, w, 0, j, j) for p, w, j in pwj}
+    near_here = {(p, w, j): hop(p, w, (3, 1)[w], j, j) for p, w, j in pwj}
+    second_sent = {(p, w, passed[w][n]): hop(p, w, (3, 1)[w], passed[w][n], 4 + n) for p, w, n in pwn}
+    second_here = {(p, w, passed[w][n]): hop(p, w, 2, passed[w][n], 4 + n) for p, w, n in pwn}
     for p in (0, 1):
         for d in (1, 3, 2):
-            spread[p, d].start()
+            spread_sent[p, d].start()
         for w in (0, 1):
-            near[p, w, 0].start()
-    nmv[...] = mine - jnp.broadcast_to(my_ratio, (8, 128)) * update
-    pltpu.make_async_copy(nmv, out_master, ow_sem.at[2]).start()
+            near_sent[p, w, 0].start()
+    out_master[...] = mine - jnp.broadcast_to(my_ratio, (8, 128)) * update
     for p in (0, 1):
         store(p, 0, 0)
     for j in (1, 3, 2):
         for p in (0, 1):
-            spread[p, 4 - j].wait_recv()
+            spread_here[p, j].wait_recv()
             for w in (0, 1):
-                near[p, w, j].start()
+                near_sent[p, w, j].start()
             store(p, 0, j)
         if j == 1:
             for p in (0, 1):
                 for w in (0, 1):
-                    near[p, w, 0].wait_recv()
+                    near_here[p, w, 0].wait_recv()
                     if 0 in passed[w]:
-                        second[p, w, 0].start()
+                        second_sent[p, w, 0].start()
                     store(p, (3, 1)[w], 0)
     for j in (1, 3, 2):
         for p in (0, 1):
             for w in (0, 1):
-                near[p, w, j].wait_recv()
+                near_here[p, w, j].wait_recv()
                 if j in passed[w]:
-                    second[p, w, j].start()
+                    second_sent[p, w, j].start()
                 store(p, (3, 1)[w], j)
     for n in (0, 1):
         for p in (0, 1):
             for w in (0, 1):
                 j = passed[w][n]
-                second[p, w, j].wait_recv()
+                second_here[p, w, j].wait_recv()
                 store(p, 2, j)
 
     for p, d in order:
@@ -303,7 +302,7 @@
     for p in (0, 1):
         for copy in ring[p]:
             copy.wait_send()
-    for group in (across, spread, near, second):
+    for group in (across, spread_sent, near_sent, second_sent):
         for copy in group.values():
             copy.wait_send()
     z_all(mz, ms_sem, mr_sem).wait_send()
@@ -311,19 +310,23 @@
     z_all(uz, us_sem, ur_sem).wait_send()
     few(ar_a, as_sem, ar_sem, zc_peer(1)).wait_send()
     few(ar_b, bs_sem, br_sem, yx_peer(1)).wait_send()
-    pltpu.make_async_copy(m1v, out_m1, ow_sem.at[0]).wait()
-    pltpu.make_async_copy(m2v, out_m2, ow_sem.at[1]).wait()
-    pltpu.make_async_copy(nmv, out_master, ow_sem.at[2]).wait()
     half = weights.at[:, :, :, c]
-    pltpu.make_async_copy(half, half, o_sem).wait()
     both = remote(half, half, ds_sem, dr_sem, {"c": other})
     both.wait_send()
     both.wait_recv()
 
 
+def write_out(*refs):
+    copies = [pltpu.make_async_copy(refs[i], refs[4 + i], refs[8].at[i]) for i in range(4)]
+    for copy in copies:
+        copy.start()
+    for copy in copies:
+        copy.wait()
+
+
 def body(grads, master, moment1, moment2, tensor_rows, step_count):
-    any_space = pl.BlockSpec(memory_space=pl.ANY)
-    smem = pl.BlockSpec(memory_space=pltpu.SMEM)
+    hbm = pl.BlockSpec(memory_space=pltpu.HBM)
+    vmem = pl.BlockSpec(memory_space=pltpu.VMEM)
     full = (NZ, NY, NX, NC, *TILE)
     block = jax.ShapeDtypeStruct(TILE, F32)
     dma = pltpu.SemaphoreType.DMA
@@ -342,31 +345,42 @@
         vm((2, 4, *TILE), F32),
         vm((NZ, *TILE), BF16),
         vm((NZ, *TILE), BF16),
+        pltpu.SMEM((NSEG,), jnp.int32),
         vm(TILE, F32),
         vm(TILE, F32),
         vm((NZ, *TILE), F32),
         vm((NZ, *TILE), F32),
         vm((16, 2, 128), F32),
         vm((16, 2, 128), F32),
-        vm(TILE, F32),
-        vm((2, 4, 4, 4, *TILE), BF16),
         dma((2, 4)), dma((2, 4)), dma((2, 4)), dma((2, 6)), dma((2, 6)), dma((2, 3)), dma((2, 3)),
         dma, dma, dma, dma, dma, dma, dma, dma, dma, dma,
-        dma((2, 3)), dma((2, 3)), dma((2, 2, 6)), dma((2, 2, 6)), dma((3,)), dma, dma, dma, dma((3,)),
+        dma((2, 3)), dma((2, 3)), dma((2, 2, 6)), dma((2, 2, 6)), dma((4,)), dma, dma,
     ]
-    weights, new_master, new_m1, new_m2 = pl.pallas_call(
+    shapes = (jax.ShapeDtypeStruct(full, BF16), block, block, block)
+    def keep(a):
+        return pltpu.with_memory_space_constraint(a, pltpu.HBM)
+
+    made = pl.pallas_call(
         kernel,
-        out_shape=(jax.ShapeDtypeStruct(full, BF16), block, block, block),
-        in_specs=[any_space] * 4 + [smem] * 2,
-        out_specs=(any_space,) * 4,
+        out_shape=shapes,
+        in_specs=[hbm] * 5 + [pl.BlockSpec(memory_space=pltpu.SMEM)],
+        out_specs=(vmem,) * 4,
         scratch_shapes=scratch,
         compiler_params=pltpu.CompilerParams(
             collective_id=0, has_side_effects=True, vmem_limit_bytes=40 * 1024 * 1024
         ),
     )(
-        grads.reshape(full), master.reshape(TILE), moment1.reshape(TILE), moment2.reshape(TILE),
-        tensor_rows, step_count,
+        keep(grads.reshape(full)), keep(master.reshape(TILE)), keep(moment1.reshape(TILE)),
+        keep(moment2.reshape(TILE)), keep(tensor_rows), step_count,
     )
+    weights, new_master, new_m1, new_m2 = pl.pallas_call(
+        write_out,
+        out_shape=shapes,
+        in_specs=[vmem] * 4,
+        out_specs=(hbm,) * 4,
+        scratch_shapes=[dma((4,))],
+        compiler_params=pltpu.CompilerParams(vmem_limit_bytes=8 * 1024 * 1024),
+    )(*made)
     return (weights.reshape(-1), new_master.reshape(-1), new_m1.reshape(-1), new_m2.reshape(-1))
 
 

time: 64.9 us -> 56.9 us (0.88)
  local copies, waits for them, and re-layouts: 8.73 us -> 0 us
  Pallas kernels: 54.6 us -> 55.5 us
    unnamed x14 -> x0, local copies, waits for them, and re-layouts: 8.73 us -> none
    pallas_call x1 -> x2, Pallas kernels: 54.6 us -> 55.5 us  [the longest x1 54 us: body(): pl.pallas_call(kernel, out_shape=shapes, in_specs=[hbm] * 5 + [pl.BlockSp...]
where the time goes in v2:
time: 56.9 us; the launch traced here: 56.8 us
  Pallas kernels  55.5 us (98%)
  between operations  1.29 us (2%)
    pallas_call x1, Pallas kernels, body(): pl.pallas_call(kernel, out_shape=shapes, in_specs=[hbm] * 5 + [pl.BlockSp...  54 us
    pallas_call x1, Pallas kernels, body(): pl.pallas_call(write_out, out_shape=shapes, in_specs=[vmem] * 4, out_spec...  1.54 us

profile of v2, /device:TPU:1, one launch (start us, length us, event | category | flops | bytes accessed | tf_op | source)
XLA Modules:
  0.0 56.8 jit_solution(17630111740939632451)
XLA Ops:
  1.3 54.0 %shard_map.93 = (bf16[8,4,4,2,5,8,128]{6,5,4,3,2,1,0:T(8,128)(2,1)S(1)}, f32[5,8,128]{2,1,0:T(8,128)S(1)}, f32[5,8,128]{2,1,0:T(8,128)S(1)}, f32[5,8,128]{2,1,0:T(8,128)S(1)}) custom-call(f32[8,4,4,2,5,8,128]{6,5,4,3,2,1,0:T(8,128)} %bitcast.8, f32[5,8,128]{2,1,0:T(8,128)} %bitcast.9, f32[5,8,128]{2,1,0:T(8,128)} %bitcast.10, f32[5,8,128]{2,1,0:T(8,128)} %bitcast.11, ...), custom_call_target="tpu_custom_call" | custom-call | tf_op jit(solution)/shard_map/pallas_call | solution.py:363
  55.3 1.5 %shard_map.94 = (bf16[8,4,4,2,5,8,128]{6,5,4,3,2,1,0:T(8,128)(2,1)}, f32[5,8,128]{2,1,0:T(8,128)}, f32[5,8,128]{2,1,0:T(8,128)}, f32[5,8,128]{2,1,0:T(8,128)}) custom-call(bf16[8,4,4,2,5,8,128]{6,5,4,3,2,1,0:T(8,128)(2,1)S(1)} %get-tuple-element.12.refs_0_, f32[5,8,128]{2,1,0:T(8,128)S(1)} %get-tuple-element.13.refs_1_, ...), custom_call_target="tpu_custom_call" | custom-call | tf_op jit(solution)/shard_map/pallas_call | solution.py:376
